TPU v7x, 32 devices: a whole 2x2x4 slice. The times are simulated.
32 devices in a mesh: win: 4 (over z), step: 8 (over y, x, core).
Axes of the slice: x: 2, y: 2, z: 4, core: 2. Of those that a mesh axis runs over, the one named last changes fastest.
Arguments:
- initial_state: float32 [32, 32, 128], replicated, may hold values from -6 to 6
- source: float32 [4, 8, 32, 32, 128], P('win', 'step'), may hold values from -6 to 6
- absorption: float32 [32, 32, 128], replicated, may hold values from 0.01 to 0.2
Outputs:
- state: float32 [4, 8, 32, 32, 128], P('win', 'step')
All inputs are finite; a program needn't handle non-finite values.
Results may differ from a plain program's by a relative error of at most 0.00026.
Values sent between devices are 32-bit elements; how exact they have to be, the bound alone decides.
A program may use at most 64 MiB of HBM per device.

v0:
```python
import functools
import math

import jax
import jax.numpy as jnp
from jax import lax
from jax.experimental import pallas as pl
from jax.experimental.pallas import tpu as pltpu
from jax.sharding import PartitionSpec as P

ITERS = 2
SWEEPS = 8


alpha_corner = 0.1
coupling = 0.05


def from_behind(block, axis, distance):
    devices = range(lax.axis_size(axis))
    route = [(i - distance, i) for i in devices if i - distance in devices]
    return lax.ppermute(block, axis, route)


def pad_cube(field):
    widths = [(0, 0)] * (field.ndim - 3) + [(1, 1)] * 3
    return jnp.pad(field, widths)


def neighbours(field):
    padded = pad_cube(field)
    total = padded[..., 2:, 1:-1, 1:-1] + padded[..., :-2, 1:-1, 1:-1]
    total = total + padded[..., 1:-1, 2:, 1:-1] + padded[..., 1:-1, :-2, 1:-1]
    total = total + padded[..., 1:-1, 1:-1, 2:] + padded[..., 1:-1, 1:-1, :-2]
    return total


def complex_times(first, second):
    return jnp.stack(
        [first[0] * second[0] - first[1] * second[1], first[0] * second[1] + first[1] * second[0]]
    )


def relax(spectrum, inverse):
    field = complex_times(inverse, spectrum)
    for repeat in range(SWEEPS - 1):
        field = complex_times(inverse, spectrum + coupling * neighbours(field))
    return field


def inverse_diagonal(angle, absorption, gamma):
    real_part = 1.0 - gamma * jnp.cos(angle) + absorption + 6.0 * coupling
    imag_part = jnp.broadcast_to(gamma * jnp.sin(angle), real_part.shape)
    magnitude = real_part * real_part + imag_part * imag_part
    return jnp.stack([real_part / magnitude, -imag_part / magnitude])


def dft_tables(window_len):
    index = jnp.arange(window_len, dtype=jnp.int32)
    product = index[:, None] * index[None, :] % window_len
    angle = product.astype(jnp.float32) * (2.0 * math.pi / window_len)
    return (jnp.cos(angle), jnp.sin(angle))


def transform_exchange(scaled, window_len):
    pencil = lax.all_to_all(scaled[None], "step", split_axis=1, concat_axis=0, tiled=True)
    cosine, sine = dft_tables(window_len)
    flat = pencil.reshape(window_len, -1)
    real_part = jnp.dot(cosine, flat, precision=lax.Precision.HIGHEST)
    imag_part = -jnp.dot(sine, flat, precision=lax.Precision.HIGHEST)
    shaped = pencil.shape
    spectrum = (
        lax.all_to_all(real_part.reshape(shaped), "step", split_axis=0, concat_axis=1, tiled=True),
        lax.all_to_all(imag_part.reshape(shaped), "step", split_axis=0, concat_axis=1, tiled=True),
    )
    return jnp.stack([spectrum[0][0], spectrum[1][0]])


def untransform_exchange(field, window_len):
    pencil = (
        lax.all_to_all(field[0][None], "step", split_axis=1, concat_axis=0, tiled=True),
        lax.all_to_all(field[1][None], "step", split_axis=1, concat_axis=0, tiled=True),
    )
    cosine, sine = dft_tables(window_len)
    shaped = pencil[0].shape
    values = jnp.dot(cosine, pencil[0].reshape(window_len, -1), precision=lax.Precision.HIGHEST)
    values = values - jnp.dot(
        sine, pencil[1].reshape(window_len, -1), precision=lax.Precision.HIGHEST
    )
    values = values / window_len
    result = lax.all_to_all(values.reshape(shaped), "step", split_axis=0, concat_axis=1, tiled=True)
    return result[0]


def per_device(initial_state, source, absorption):
    window_len = lax.axis_size("step")
    moment = lax.axis_index("step")
    window_index = lax.axis_index("win")
    gamma = alpha_corner ** (1.0 / window_len)
    scale = gamma ** moment.astype(jnp.float32)
    forcing_base = source[0, 0]
    is_first = moment == 0
    state = jnp.zeros_like(forcing_base)
    angle = moment.astype(jnp.float32) * (2.0 * math.pi / window_len)
    inverse = inverse_diagonal(angle, absorption, gamma)
    for repeat in range(ITERS):
        if repeat == 0:
            correction = jnp.where(window_index == 0, initial_state, 0.0)
        else:
            ends = from_behind(state, "step", 1 - window_len)
            before = from_behind(ends, "win", 1)
            before = jnp.where(window_index == 0, initial_state, before)
            correction = before - alpha_corner * ends
        forcing = forcing_base + jnp.where(is_first, correction, 0.0)
        scaled = forcing * scale
        spectrum = transform_exchange(scaled, window_len)
        field = relax(spectrum, inverse)
        values = untransform_exchange(field, window_len)
        state = values / scale
    return state[None, None]


LANES = 128
TILE = 8


def tables(length):
    gamma = alpha_corner ** (1.0 / length)
    into, back, angles = [], [], []
    for core in range(2):
        rows_in, rows_back = [], []
        for time in range(length):
            scale = gamma**time
            row_in, row_back = [], []
            for p in range(length // 4):
                j = 2 * p + core
                if j == 0:
                    pair, weight = (1.0, (-1.0) ** time), 1.0 / length
                else:
                    turn = 2.0 * math.pi * (j * time % length) / length
                    pair, weight = (math.cos(turn), -math.sin(turn)), 2.0 / length
                row_in += [value * scale / coupling for value in pair]
                row_back += [value * weight / scale for value in pair]
            rows_in.append(row_in)
            rows_back.append(row_back)
        into.append(rows_in)
        back.append(rows_back)
        angles.append([2.0 * math.pi * (2 * p + core) / length for p in range(length // 4)])
    return into, back, angles


def kernel(
    length, windows, nx, ny, ext, ey,
    source, initial, absorb, out,
    raw, first, absv, coef, base, fa, fb, corr,
    psend, pgot, ends, zgot, csend, qsend, qgot, obuf,
    lsem, asend, brecv, fsend, esem, zsem, csem_s, csem_r, qsem_s, qsem_r, osem_s, osem_r,
):
    half = length // 2
    gx, gy = half // 2, 2
    bs, bsy = nx // gx, ny // gy
    reach = SWEEPS - 1
    pairs = length // 4
    units = 2 * pairs
    gamma = alpha_corner ** (1.0 / length)
    into, back, angles = tables(length)
    me = lax.axis_index("step")
    w = lax.axis_index("win")
    core, m = me % 2, me // 2
    partner = m * 2 + (1 - core)
    bx, by = m % gx, m // gx

    def xlo(b):
        if gx == 2:
            return b * (nx - ext)
        return jnp.minimum(jnp.maximum(b * bs - reach, 0), nx - ext)

    def ylo(b):
        return pl.multiple_of(b * (ny - ey), TILE)

    def pick(a, b):
        return jnp.where(core == 0, jnp.float32(a), jnp.float32(b))

    def region(ref, b_x, b_y):
        return ref.at[pl.ds(xlo(b_x), ext), pl.ds(ylo(b_y), ey), :]

    ox = bx * bs - xlo(bx)
    oy = pl.multiple_of(by * bsy - ylo(by), TILE)

    loads = [
        pltpu.make_async_copy(region(absorb, bx, by), absv, lsem.at[0]),
        pltpu.make_async_copy(region(source, bx, by), raw.at[me], lsem.at[1]),
        pltpu.make_async_copy(region(initial, bx, by), first, lsem.at[2]),
    ]
    for load in loads:
        load.start()
    zero_row = jnp.zeros((ey, LANES), jnp.float32)
    for u in range(units):
        for ref in (fa, fb):
            ref[u, 0] = zero_row
            ref[u, ext + 1] = zero_row
    if gx > 2:
        corr[...] = jnp.zeros_like(corr)

    barrier = pltpu.get_barrier_semaphore()
    for d in range(1, length):
        pl.semaphore_signal(
            barrier, inc=1, device_id={"step": (me + d) % length}, device_id_type=pl.DeviceIdType.MESH
        )

    @pl.when(w > 0)
    def _():
        pl.semaphore_signal(barrier, inc=1, device_id={"win": w - 1}, device_id_type=pl.DeviceIdType.MESH)

    @pl.when(w < windows - 1)
    def _():
        pl.semaphore_signal(barrier, inc=1, device_id={"win": w + 1}, device_id_type=pl.DeviceIdType.MESH)

    nearby = jnp.where(w > 0, 1, 0) + jnp.where(w < windows - 1, 1, 0)
    pl.semaphore_wait(barrier, length - 1 + nearby)

    def remote(src, dst, send, recv, **where):
        return pltpu.make_async_remote_copy(
            src_ref=src, dst_ref=dst, send_sem=send, recv_sem=recv,
            device_id=where, device_id_type=pl.DeviceIdType.MESH,
        )

    outgoing = []
    for d in range(1, half):
        to = (m + d) % half
        copy = remote(
            region(source, to % gx, to // gx), raw.at[me], asend.at[d], brecv.at[me], step=to * 2 + core
        )
        copy.start()
        outgoing.append(copy)
    copy = remote(region(source, bx, by), raw.at[me], asend.at[0], brecv.at[me], step=partner)
    copy.start()
    outgoing.append(copy)

    loads[0].wait()

    def coefficients(i, carry):
        for p in range(pairs):
            rows = absv[i]
            cosine = pick(math.cos(angles[0][p]), math.cos(angles[1][p]))
            imag = pick(gamma * math.sin(angles[0][p]), gamma * math.sin(angles[1][p]))
            real = 1.0 - gamma * cosine + rows + 6.0 * coupling
            over = coupling / (real * real + imag * imag)
            coef[3 * p, i] = real * over
            coef[3 * p + 1, i] = -imag * over
            if p == 0:
                other = pick(-1.0, math.cos(angles[1][p]))
                real = 1.0 - gamma * other + rows + 6.0 * coupling
                over = coupling / (real * real + imag * imag)
                coef[3 * p + 2, i] = real * over
        return carry

    lax.fori_loop(0, ext, coefficients, 0)

    def weights(p, i):
        straight = coef[3 * p, i]
        return straight, (coef[3 * p + 2, i] if p == 0 else straight), coef[3 * p + 1, i]

    def arrival(t):
        return remote(raw.at[t], raw.at[t], asend.at[0], brecv.at[t], step=partner)

    for d in range(1, half):
        t = ((m + half - d) % half) * 2 + core
        arrival(t).wait_recv()
        copy = remote(raw.at[t], raw.at[t], fsend.at[d], brecv.at[t], step=partner)
        copy.start()
        outgoing.append(copy)
    for d in range(half):
        arrival(((m + half - d) % half) * 2 + (1 - core)).wait_recv()
    loads[1].wait()
    loads[2].wait()
    is_first = jnp.where(w == 0, jnp.float32(1.0 / coupling), jnp.float32(0.0))

    def second_weight(p, weight):
        return weight[2] + (pick(1.0, 0.0) * weight[1] if p == 0 else 0.0)

    def transform(i, carry):
        begin = first[i] * is_first
        fields = [raw[t, i] for t in range(length)]
        for p in range(pairs):
            weight = weights(p, i)
            s0, s1 = begin, begin * pick(1.0, 0.0) if p == 0 else None
            for t in range(length):
                s0 = s0 + pick(into[0][t][2 * p], into[1][t][2 * p]) * fields[t]
                term = pick(into[0][t][2 * p + 1], into[1][t][2 * p + 1]) * fields[t]
                s1 = term if s1 is None else s1 + term
            b0 = weight[0] * s0 - weight[2] * s1
            b1 = weight[1] * s1 + weight[2] * s0
            base[2 * p, i] = b0
            base[2 * p + 1, i] = b1
            fa[2 * p, i + 1] = b0
            fa[2 * p + 1, i + 1] = b1
        return carry

    lax.fori_loop(0, ext, transform, 0)

    lane = lax.broadcasted_iota(jnp.int32, (ey, LANES), 1)
    row = lax.broadcasted_iota(jnp.int32, (ey, LANES), 0)

    def around(ref, u, r):
        v = ref[u, r]
        total = ref[u, r - 1] + ref[u, r + 1]
        total = total + jnp.where(lane == 0, 0.0, pltpu.roll(v, 1, 1))
        total = total + jnp.where(lane == LANES - 1, 0.0, pltpu.roll(v, LANES - 1, 1))
        total = total + jnp.where(row == 0, 0.0, pltpu.roll(v, 1, 0))
        total = total + jnp.where(row == ey - 1, 0.0, pltpu.roll(v, ey - 1, 0))
        return total

    def sweeps():
        here, there = fa, fb
        for k in range(1, SWEEPS):
            begin, count = (bx * k, ext - k) if gx == 2 else (0, ext)

            def body(n, carry, here=here, there=there, begin=begin):
                i = begin + n
                for p in range(pairs):
                    weight = weights(p, i)
                    n0 = around(here, 2 * p, i + 1)
                    n1 = around(here, 2 * p + 1, i + 1)
                    there[2 * p, i + 1] = base[2 * p, i] + (weight[0] * n0 - weight[2] * n1)
                    there[2 * p + 1, i + 1] = base[2 * p + 1, i] + (weight[1] * n1 + weight[2] * n0)
                return carry

            lax.fori_loop(0, count, body, 0)
            here, there = there, here
        return here

    final = sweeps()

    def part(t, y0, rows):
        total = None
        for u in range(units):
            factor = pick(back[0][t[0]][u], back[1][t[1]][u])
            term = factor * final[u, pl.ds(ox + 1, bs), pl.ds(y0, rows), :]
            total = term if total is None else total + term
        return total

    last = (length - 1, length - 1)
    psend[...] = part(last, pl.multiple_of(oy + TILE * (1 - core), TILE), TILE)
    swap = remote(psend, pgot, esem.at[0], esem.at[1], step=partner)
    swap.start()
    mine = part(last, pl.multiple_of(oy + TILE * core, TILE), TILE)
    swap.wait_recv()
    mine = mine + pgot[...]
    ends[...] = mine
    outgoing.append(swap)

    onward = remote(ends, zgot, zsem.at[0], zsem.at[1], win=(w + 1) % windows)

    @pl.when(w < windows - 1)
    def _():
        onward.start()

    @pl.when(w == 0)
    def _():
        zgot[...] = jnp.zeros_like(zgot)

    @pl.when(w > 0)
    def _():
        onward.wait_recv()

    change = zgot[...] - alpha_corner * ends[...]
    csend[...] = change
    corr[pl.ds(ox, bs), pl.ds(pl.multiple_of(oy + TILE * core, TILE), TILE), :] = change

    def spread(ex, ey_, send):
        rows, skip = (bs, 0) if ex == 0 else (reach, bs - reach if ex == 1 else 0)
        tx, ty = (bx + ex, by + ey_) if send else (bx, by)
        fx, fy = (bx, by) if send else (bx - ex, by - ey_)
        ax, ay = (tx, ty) if send else (fx, fy)
        inside = (ax >= 0) & (ax < gx) & (ay >= 0) & (ay < gy)
        slot = ((ex + 1) * 3 + (ey_ + 1)) * 2
        for c in range(2):
            near = c == (1 if ey_ == 1 else 0)
            if send:
                okay = inside if ey_ == 0 else inside & (core == (1 if ey_ == 1 else 0))
                if ex == 0 and ey_ == 0:
                    okay = core != c
                fc, tc = core, c
            else:
                if ey_ != 0 and not near:
                    continue
                okay = inside
                if ex == 0 and ey_ == 0:
                    okay = core != c
                fc, tc = c, core

            @pl.when(okay)
            def _(c=c, fc=fc, tc=tc):
                copy = remote(
                    csend.at[pl.ds(skip, rows)],
                    corr.at[
                        pl.ds(fx * bs + skip - xlo(tx), rows),
                        pl.ds(pl.multiple_of(fy * bsy + TILE * fc - ylo(ty), TILE), TILE),
                        :,
                    ],
                    csem_s.at[slot + c],
                    csem_r.at[slot + fc],
                    step=(ty * gx + tx) * 2 + tc if send == 1 else partner,
                )
                if send == 1:
                    copy.start()
                elif send == 2:
                    copy.wait_send()
                else:
                    copy.wait_recv()

    offsets = [(ex, e) for ex in (-1, 0, 1) for e in (-1, 0, 1)]
    for ex, e in offsets:
        spread(ex, e, 1)
    for ex, e in offsets:
        spread(ex, e, 0)

    def correct(i, carry):
        x = corr[i] * (1.0 / coupling)
        for p in range(pairs):
            weight = weights(p, i)
            b0 = base[2 * p, i] + weight[0] * x
            b1 = base[2 * p + 1, i] + second_weight(p, weight) * x
            base[2 * p, i] = b0
            base[2 * p + 1, i] = b1
            fa[2 * p, i + 1] = b0
            fa[2 * p + 1, i + 1] = b1
        return carry

    lax.fori_loop(0, ext, correct, 0)
    final = sweeps()

    for k in range(half):
        qsend[k] = part((2 * k + 1, 2 * k), oy, bsy)
        copy = remote(qsend.at[k], qgot.at[k], qsem_s.at[k], qsem_r.at[k], step=partner)
        copy.start()
        outgoing.append(copy)
    for k in range(half):
        obuf[k] = part((2 * k, 2 * k + 1), oy, bsy)

    def place(b_x, b_y):
        return out.at[pl.ds(b_x * bs, bs), pl.ds(pl.multiple_of(b_y * bsy, TILE), bsy), :]

    for k in range(half):
        remote(qsend.at[k], qgot.at[k], qsem_s.at[k], qsem_r.at[k], step=partner).wait_recv()
        obuf[k] = obuf[k] + qgot[k]

        @pl.when(m == k)
        def _(k=k):
            pltpu.make_async_copy(obuf.at[k], place(bx, by), lsem.at[3]).start()

        @pl.when(m != k)
        def _(k=k):
            remote(obuf.at[k], place(bx, by), osem_s.at[k], osem_r.at[m], step=2 * k + core).start()

    for copy in outgoing:
        copy.wait_send()
    for ex, e in offsets:
        spread(ex, e, 2)

    @pl.when(w < windows - 1)
    def _():
        onward.wait_send()

    for k in range(half):

        @pl.when(m == k)
        def _(k=k):
            pltpu.make_async_copy(obuf.at[k], place(bx, by), lsem.at[3]).wait()

        @pl.when(m != k)
        def _(k=k):
            done = remote(obuf.at[k], place(k % gx, k // gx), osem_s.at[k], osem_r.at[k], step=partner)
            done.wait_send()
            done.wait_recv()


def blocks(initial_state, source, absorption):
    length = lax.axis_size("step")
    windows = lax.axis_size("win")
    nx, ny, nz = initial_state.shape
    half = length // 2
    gx, reach = half // 2, SWEEPS - 1
    bs, bsy = nx // gx, ny // 2
    ext = min(nx, bs + reach * (1 if gx == 2 else 2))
    ey = bsy + -(-reach // TILE) * TILE
    units = length // 2
    f32 = jnp.float32
    dma = pltpu.SemaphoreType.DMA
    return pl.pallas_call(
        functools.partial(kernel, length, windows, nx, ny, ext, ey),
        out_shape=jax.ShapeDtypeStruct((nx, ny, nz), f32),
        in_specs=[pl.BlockSpec(memory_space=pl.ANY)] * 3,
        out_specs=pl.BlockSpec(memory_space=pl.ANY),
        scratch_shapes=[
            pltpu.VMEM((length, ext, ey, nz), f32),
            pltpu.VMEM((ext, ey, nz), f32),
            pltpu.VMEM((ext, ey, nz), f32),
            pltpu.VMEM((3 * length // 4, ext, ey, nz), f32),
            pltpu.VMEM((units, ext, ey, nz), f32),
            pltpu.VMEM((units, ext + 2, ey, nz), f32),
            pltpu.VMEM((units, ext + 2, ey, nz), f32),
            pltpu.VMEM((ext, ey, nz), f32),
            pltpu.VMEM((bs, TILE, nz), f32),
            pltpu.VMEM((bs, TILE, nz), f32),
            pltpu.VMEM((bs, TILE, nz), f32),
            pltpu.VMEM((bs, TILE, nz), f32),
            pltpu.VMEM((bs, TILE, nz), f32),
            pltpu.VMEM((half, bs, bsy, nz), f32),
            pltpu.VMEM((half, bs, bsy, nz), f32),
            pltpu.VMEM((half, bs, bsy, nz), f32),
            dma((4,)),
            dma((half,)),
            dma((length,)),
            dma((half,)),
            dma((2,)),
            dma((2,)),
            dma((18,)),
            dma((18,)),
            dma((half,)),
            dma((half,)),
            dma((half,)),
            dma((half,)),
        ],
        compiler_params=pltpu.CompilerParams(
            collective_id=0, has_side_effects=True, vmem_limit_bytes=60 * 1024 * 1024
        ),
    )(source[0, 0], initial_state, absorption)[None, None]


def fits(mesh, shape):
    length = mesh.shape["step"]
    if length % 8 or shape[2] != LANES or shape[1] != 4 * TILE:
        return False
    gx = length // 4
    return shape[0] % gx == 0 and shape[0] // gx >= SWEEPS - 1


def solution(mesh):
    def body(initial_state, source, absorption):
        plan = blocks if fits(mesh, initial_state.shape) else per_device
        return plan(initial_state, source, absorption)

    return jax.shard_map(
        body,
        mesh=mesh,
        in_specs=(P(), P("win", "step", None, None, None), P()),
        out_specs=P("win", "step", None, None, None),
        check_vma=False,
    )
```

profile of v0, /device:TPU:12, one launch (start us, length us, event | category | flops | bytes accessed | tf_op | source)
XLA Modules:
  0.0 65.8 jit_solution(5269717601556103201)
XLA Ops:
  0.0 63.9 %shard_map.37 = f32[32,32,128]{2,1,0:T(8,128)} custom-call(f32[32,32,128]{2,1,0:T(8,128)} %bitcast.3, f32[32,32,128]{2,1,0:T(8,128)} %initial.1, f32[32,32,128]{2,1,0:T(8,128)} %absorb.1), custom_call_target="tpu_custom_call" | custom-call | tf_op jit(solution)/shard_map/pallas_call | solution.py:491
  63.9 1.9 %copy.5 = f32[1,1,32,32,128]{4,3,2,1,0:T(8,128)} copy(f32[1,1,32,32,128]{4,3,2,1,0:T(8,128)} %bitcast.2) | data formatting | bytes 1048576
where the time goes:
time: 66 us; the launch traced here: 65.8 us
  Pallas kernels  63.9 us (97%)
  local copies, waits for them, and re-layouts  1.87 us (3%)
    pallas_call x1, Pallas kernels, blocks(): pl.pallas_call(functools.partial(kernel, length, windows, nx, ny, ext, ey...  63.9 us
    unnamed x1, local copies, waits for them, and re-layouts  1.87 us

commit v1 on v0

--- a/solution.py
+++ b/solution.py
@@ -122,6 +122,7 @@
 
 LANES = 128
 TILE = 8
+GROUP = 8
 
 
 def tables(length):
@@ -152,7 +153,7 @@
 def kernel(
     length, windows, nx, ny, ext, ey,
     source, initial, absorb, out,
-    raw, first, absv, coef, base, fa, fb, corr,
+    raw, first, absv, coef, base, again, fa, fb, corr,
     psend, pgot, ends, zgot, csend, qsend, qgot, obuf,
     lsem, asend, brecv, fsend, esem, zsem, csem_s, csem_r, qsem_s, qsem_r, osem_s, osem_r,
 ):
@@ -197,8 +198,11 @@
     zero_row = jnp.zeros((ey, LANES), jnp.float32)
     for u in range(units):
         for ref in (fa, fb):
-            ref[u, 0] = zero_row
-            ref[u, ext + 1] = zero_row
+            ref[u, 0, pl.ds(TILE, ey)] = zero_row
+            ref[u, ext + 1, pl.ds(TILE, ey)] = zero_row
+            for r in range(1, ext + 1):
+                ref[u, r, pl.ds(0, TILE)] = zero_row[:TILE]
+                ref[u, r, pl.ds(TILE + ey, TILE)] = zero_row[:TILE]
     if gx > 2:
         corr[...] = jnp.zeros_like(corr)
 
@@ -237,9 +241,27 @@
     copy.start()
     outgoing.append(copy)
 
+    def grouped(begin, count, work, most=GROUP):
+        size = min(most, count)
+
+        def body(g, carry):
+            work(begin + g * size, size)
+            return carry
+
+        lax.fori_loop(0, count // size, body, 0)
+        if count % size:
+            work(begin + count - size, size)
+
+    def each(one):
+        def work(start, rows):
+            for n in range(rows):
+                one(start + n)
+
+        return work
+
     loads[0].wait()
 
-    def coefficients(i, carry):
+    def coefficients(i):
         for p in range(pairs):
             rows = absv[i]
             cosine = pick(math.cos(angles[0][p]), math.cos(angles[1][p]))
@@ -253,9 +275,8 @@
                 real = 1.0 - gamma * other + rows + 6.0 * coupling
                 over = coupling / (real * real + imag * imag)
                 coef[3 * p + 2, i] = real * over
-        return carry
-
-    lax.fori_loop(0, ext, coefficients, 0)
+
+    grouped(0, ext, each(coefficients))
 
     def weights(p, i):
         straight = coef[3 * p, i]
@@ -279,7 +300,7 @@
     def second_weight(p, weight):
         return weight[2] + (pick(1.0, 0.0) * weight[1] if p == 0 else 0.0)
 
-    def transform(i, carry):
+    def transform(i):
         begin = first[i] * is_first
         fields = [raw[t, i] for t in range(length)]
         for p in range(pairs):
@@ -293,50 +314,47 @@
             b1 = weight[1] * s1 + weight[2] * s0
             base[2 * p, i] = b0
             base[2 * p + 1, i] = b1
-            fa[2 * p, i + 1] = b0
-            fa[2 * p + 1, i + 1] = b1
-        return carry
-
-    lax.fori_loop(0, ext, transform, 0)
+            fa[2 * p, i + 1, pl.ds(TILE, ey)] = b0
+            fa[2 * p + 1, i + 1, pl.ds(TILE, ey)] = b1
+
+    grouped(0, ext, each(transform), GROUP // 2)
 
     lane = lax.broadcasted_iota(jnp.int32, (ey, LANES), 1)
-    row = lax.broadcasted_iota(jnp.int32, (ey, LANES), 0)
 
     def around(ref, u, r):
-        v = ref[u, r]
-        total = ref[u, r - 1] + ref[u, r + 1]
-        total = total + jnp.where(lane == 0, 0.0, pltpu.roll(v, 1, 1))
+        v = ref[u, r, pl.ds(TILE, ey)]
+        total = jnp.where(lane == 0, 0.0, pltpu.roll(v, 1, 1))
         total = total + jnp.where(lane == LANES - 1, 0.0, pltpu.roll(v, LANES - 1, 1))
-        total = total + jnp.where(row == 0, 0.0, pltpu.roll(v, 1, 0))
-        total = total + jnp.where(row == ey - 1, 0.0, pltpu.roll(v, ey - 1, 0))
-        return total
-
-    def sweeps():
+        beside = ref[u, r - 1, pl.ds(TILE, ey)] + ref[u, r + 1, pl.ds(TILE, ey)]
+        return total + (beside + (ref[u, r, pl.ds(TILE - 1, ey)] + ref[u, r, pl.ds(TILE + 1, ey)]))
+
+    def sweep_rows(base, here, there, start, rows):
+        for n in range(rows):
+            i = start + n
+            for p in range(pairs):
+                weight = weights(p, i)
+                n0 = around(here, 2 * p, i + 1)
+                n1 = around(here, 2 * p + 1, i + 1)
+                there[2 * p, i + 1, pl.ds(TILE, ey)] = base[2 * p, i] + (weight[0] * n0 - weight[2] * n1)
+                there[2 * p + 1, i + 1, pl.ds(TILE, ey)] = base[2 * p + 1, i] + (
+                    weight[1] * n1 + weight[2] * n0
+                )
+
+    def sweeps(base):
         here, there = fa, fb
         for k in range(1, SWEEPS):
             begin, count = (bx * k, ext - k) if gx == 2 else (0, ext)
-
-            def body(n, carry, here=here, there=there, begin=begin):
-                i = begin + n
-                for p in range(pairs):
-                    weight = weights(p, i)
-                    n0 = around(here, 2 * p, i + 1)
-                    n1 = around(here, 2 * p + 1, i + 1)
-                    there[2 * p, i + 1] = base[2 * p, i] + (weight[0] * n0 - weight[2] * n1)
-                    there[2 * p + 1, i + 1] = base[2 * p + 1, i] + (weight[1] * n1 + weight[2] * n0)
-                return carry
-
-            lax.fori_loop(0, count, body, 0)
+            grouped(begin, count, functools.partial(sweep_rows, base, here, there))
             here, there = there, here
         return here
 
-    final = sweeps()
+    final = sweeps(base)
 
     def part(t, y0, rows):
         total = None
         for u in range(units):
             factor = pick(back[0][t[0]][u], back[1][t[1]][u])
-            term = factor * final[u, pl.ds(ox + 1, bs), pl.ds(y0, rows), :]
+            term = factor * final[u, pl.ds(ox + 1, bs), pl.ds(y0 + TILE, rows), :]
             total = term if total is None else total + term
         return total
 
@@ -416,20 +434,19 @@
     for ex, e in offsets:
         spread(ex, e, 0)
 
-    def correct(i, carry):
+    def correct(i):
         x = corr[i] * (1.0 / coupling)
         for p in range(pairs):
             weight = weights(p, i)
             b0 = base[2 * p, i] + weight[0] * x
             b1 = base[2 * p + 1, i] + second_weight(p, weight) * x
-            base[2 * p, i] = b0
-            base[2 * p + 1, i] = b1
-            fa[2 * p, i + 1] = b0
-            fa[2 * p + 1, i + 1] = b1
-        return carry
-
-    lax.fori_loop(0, ext, correct, 0)
-    final = sweeps()
+            again[2 * p, i] = b0
+            again[2 * p + 1, i] = b1
+            fa[2 * p, i + 1, pl.ds(TILE, ey)] = b0
+            fa[2 * p + 1, i + 1, pl.ds(TILE, ey)] = b1
+
+    grouped(0, ext, each(correct))
+    final = sweeps(again)
 
     for k in range(half):
         qsend[k] = part((2 * k + 1, 2 * k), oy, bsy)
@@ -499,8 +516,9 @@
             pltpu.VMEM((ext, ey, nz), f32),
             pltpu.VMEM((3 * length // 4, ext, ey, nz), f32),
             pltpu.VMEM((units, ext, ey, nz), f32),
-            pltpu.VMEM((units, ext + 2, ey, nz), f32),
-            pltpu.VMEM((units, ext + 2, ey, nz), f32),
+            pltpu.VMEM((units, ext, ey, nz), f32),
+            pltpu.VMEM((units, ext + 2, ey + 2 * TILE, nz), f32),
+            pltpu.VMEM((units, ext + 2, ey + 2 * TILE, nz), f32),
             pltpu.VMEM((ext, ey, nz), f32),
             pltpu.VMEM((bs, TILE, nz), f32),
             pltpu.VMEM((bs, TILE, nz), f32),
@@ -524,7 +542,7 @@
             dma((half,)),
         ],
         compiler_params=pltpu.CompilerParams(
-            collective_id=0, has_side_effects=True, vmem_limit_bytes=60 * 1024 * 1024
+            collective_id=0, has_side_effects=True, vmem_limit_bytes=28 * 1024 * 1024
         ),
     )(source[0, 0], initial_state, absorption)[None, None]
 

time: 66 us -> 52.3 us (0.79)
  Pallas kernels: 63.9 us -> 48.1 us
  local copies, waits for them, and re-layouts: 1.87 us -> 3.92 us
    pallas_call x1, Pallas kernels: 63.9 us -> 48.1 us  [blocks(): pl.pallas_call(functools.partial(kernel, length, windows, nx, ny, ext, ey...]
    unnamed x1 -> x7, local copies, waits for them, and re-layouts: 1.87 us -> 3.92 us
where the time goes in v1:
time: 52.3 us; the launch traced here: 52.1 us
  Pallas kernels  48.1 us (92%)
  local copies, waits for them, and re-layouts  3.92 us (7%)
    pallas_call x1, Pallas kernels, blocks(): pl.pallas_call(functools.partial(kernel, length, windows, nx, ny, ext, ey...  48.1 us
    unnamed x7, local copies, waits for them, and re-layouts  3.92 us

profile of v1, /device:TPU:12, one launch (start us, length us, event | category | flops | bytes accessed | tf_op | source)
XLA Modules:
  0.0 52.1 jit_solution(5468250186293458456)
XLA Ops:
  0.0 0.0 copy-start
  0.0 1.0 %copy-done = f32[1,1,32,32,128]{4,3,2,1,0:T(8,128)S(1)} copy-done((f32[1,1,32,32,128]{4,3,2,1,0:T(8,128)S(1)}, f32[1,1,32,32,128]{4,3,2,1,0:T(8,128)}, u32[]{:S(2)}) %copy-start) | copy-done | bytes 524312
  1.0 0.0 copy-start.1
  1.0 1.0 %copy-done.1 = f32[32,32,128]{2,1,0:T(8,128)S(1)} copy-done((f32[32,32,128]{2,1,0:T(8,128)S(1)}, f32[32,32,128]{2,1,0:T(8,128)}, u32[]{:S(2)}) %copy-start.1) | copy-done | bytes 524312
  2.1 0.0 copy-start.2
  2.1 1.0 %copy-done.2 = f32[32,32,128]{2,1,0:T(8,128)S(1)} copy-done((f32[32,32,128]{2,1,0:T(8,128)S(1)}, f32[32,32,128]{2,1,0:T(8,128)}, u32[]{:S(2)}) %copy-start.2) | copy-done | bytes 524312
  3.1 48.1 %shard_map.37 = f32[32,32,128]{2,1,0:T(8,128)S(1)} custom-call(f32[32,32,128]{2,1,0:T(8,128)S(1)} %bitcast.3, f32[32,32,128]{2,1,0:T(8,128)S(1)} %copy-done.1, f32[32,32,128]{2,1,0:T(8,128)S(1)} %copy-done.2), custom_call_target="tpu_custom_call" | custom-call | tf_op jit(solution)/shard_map/pallas_call | solution.py:508
  51.3 0.8 %copy.5 = f32[1,1,32,32,128]{4,3,2,1,0:T(8,128)} copy(f32[1,1,32,32,128]{4,3,2,1,0:T(8,128)S(1)} %bitcast.2) | data formatting | bytes 1048576
Async XLA Ops:
  0.0 1.0 %copy-start = (f32[1,1,32,32,128]{4,3,2,1,0:T(8,128)S(1)}, f32[1,1,32,32,128]{4,3,2,1,0:T(8,128)}, u32[]{:S(2)}) copy-start(f32[1,1,32,32,128]{4,3,2,1,0:T(8,128)} %param.4) | copy-start | bytes 1572868
  1.0 1.0 %copy-start.1 = (f32[32,32,128]{2,1,0:T(8,128)S(1)}, f32[32,32,128]{2,1,0:T(8,128)}, u32[]{:S(2)}) copy-start(f32[32,32,128]{2,1,0:T(8,128)} %initial.1) | copy-start | bytes 1572868
  2.1 1.0 %copy-start.2 = (f32[32,32,128]{2,1,0:T(8,128)S(1)}, f32[32,32,128]{2,1,0:T(8,128)}, u32[]{:S(2)}) copy-start(f32[32,32,128]{2,1,0:T(8,128)} %absorb.1) | copy-start | bytes 1572868

commit v2 on v1

--- a/solution.py
+++ b/solution.py
@@ -242,7 +242,7 @@
     outgoing.append(copy)
 
     def grouped(begin, count, work, most=GROUP):
-        size = min(most, count)
+        size = -(-count // max(1, count // most))
 
         def body(g, carry):
             work(begin + g * size, size)

time: 52.3 us -> 49.8 us (0.952)
  Pallas kernels: 48.1 us -> 45.6 us
    pallas_call x1, Pallas kernels: 48.1 us -> 45.6 us  [blocks(): pl.pallas_call(functools.partial(kernel, length, windows, nx, ny, ext, ey...]
where the time goes in v2:
time: 49.8 us; the launch traced here: 49.6 us
  Pallas kernels  45.6 us (92%)
  local copies, waits for them, and re-layouts  3.92 us (8%)
    pallas_call x1, Pallas kernels, blocks(): pl.pallas_call(functools.partial(kernel, length, windows, nx, ny, ext, ey...  45.6 us
    unnamed x7, local copies, waits for them, and re-layouts  3.92 us

profile of v2, /device:TPU:12, one launch (start us, length us, event | category | flops | bytes accessed | tf_op | source)
XLA Modules:
  0.0 49.6 jit_solution(10076711884944219785)
XLA Ops:
  0.0 0.0 copy-start
  0.0 1.0 %copy-done = f32[1,1,32,32,128]{4,3,2,1,0:T(8,128)S(1)} copy-done((f32[1,1,32,32,128]{4,3,2,1,0:T(8,128)S(1)}, f32[1,1,32,32,128]{4,3,2,1,0:T(8,128)}, u32[]{:S(2)}) %copy-start) | copy-done | bytes 524312
  1.0 0.0 copy-start.1
  1.0 1.0 %copy-done.1 = f32[32,32,128]{2,1,0:T(8,128)S(1)} copy-done((f32[32,32,128]{2,1,0:T(8,128)S(1)}, f32[32,32,128]{2,1,0:T(8,128)}, u32[]{:S(2)}) %copy-start.1) | copy-done | bytes 524312
  2.1 0.0 copy-start.2
  2.1 1.0 %copy-done.2 = f32[32,32,128]{2,1,0:T(8,128)S(1)} copy-done((f32[32,32,128]{2,1,0:T(8,128)S(1)}, f32[32,32,128]{2,1,0:T(8,128)}, u32[]{:S(2)}) %copy-start.2) | copy-done | bytes 524312
  3.1 45.6 %shard_map.37 = f32[32,32,128]{2,1,0:T(8,128)S(1)} custom-call(f32[32,32,128]{2,1,0:T(8,128)S(1)} %bitcast.3, f32[32,32,128]{2,1,0:T(8,128)S(1)} %copy-done.1, f32[32,32,128]{2,1,0:T(8,128)S(1)} %copy-done.2), custom_call_target="tpu_custom_call" | custom-call | tf_op jit(solution)/shard_map/pallas_call | solution.py:508
  48.8 0.8 %copy.5 = f32[1,1,32,32,128]{4,3,2,1,0:T(8,128)} copy(f32[1,1,32,32,128]{4,3,2,1,0:T(8,128)S(1)} %bitcast.2) | data formatting | bytes 1048576
Async XLA Ops:
  0.0 1.0 %copy-start = (f32[1,1,32,32,128]{4,3,2,1,0:T(8,128)S(1)}, f32[1,1,32,32,128]{4,3,2,1,0:T(8,128)}, u32[]{:S(2)}) copy-start(f32[1,1,32,32,128]{4,3,2,1,0:T(8,128)} %param.4) | copy-start | bytes 1572868
  1.0 1.0 %copy-start.1 = (f32[32,32,128]{2,1,0:T(8,128)S(1)}, f32[32,32,128]{2,1,0:T(8,128)}, u32[]{:S(2)}) copy-start(f32[32,32,128]{2,1,0:T(8,128)} %initial.1) | copy-start | bytes 1572868
  2.1 1.0 %copy-start.2 = (f32[32,32,128]{2,1,0:T(8,128)S(1)}, f32[32,32,128]{2,1,0:T(8,128)}, u32[]{:S(2)}) copy-start(f32[32,32,128]{2,1,0:T(8,128)} %absorb.1) | copy-start | bytes 1572868
